TPU v7x, 32 devices: a whole 2x2x4 slice. The times are simulated.
32 devices in a mesh: group: 4 (over y, x), dev: 8 (over z, core).
Axes of the slice: x: 2, y: 2, z: 4, core: 2. Of those that a mesh axis runs over, the one named last changes fastest.
Arguments:
- fluid_state: float32 [4, 4, 16, 128, 128], P('group', None, None, 'dev'), may hold values from -6 to 6
- coupling: float32 [4, 4], replicated, may hold values from -2.5 to 2.5
- displacement: float32 [3, 32768], P(None, 'dev'), may hold values from -6 to 6
- slot_cells: int32 [4, 8, 8, 8, 128], P('group', 'dev'), may hold values from 0 to 32767
- slot_weights: float32 [4, 8, 8, 8, 128], P('group', 'dev'), may hold values from 0.05 to 0.25
- slot_nodes: int32 [4, 8, 8, 128], P('group', 'dev'), may hold values from 0 to 4095
- slot_counts: int32 [4, 8, 8], P('group', 'dev'), may hold values from 1 to 128, as said below
- flexibility: float32 [24, 24, 4096], P(None, None, 'dev'), may hold values from -1.25 to 1.25
- resid_prev: float32 [3, 32768], P(None, 'dev'), may hold values from -520 to 520
- struct_prev: float32 [3, 32768], P(None, 'dev'), may hold values from -6 to 6
- v_hist: float32 [7, 3, 32768], P(None, None, 'dev'), may hold values from -80 to 80
- w_hist: float32 [7, 3, 32768], P(None, None, 'dev'), may hold values from -6 to 6
Outputs:
- fluid_out: float32 [4, 4, 16, 128, 128], P('group', None, None, 'dev')
- updated: float32 [3, 32768], P(None, 'dev')
Inputs may be any that keep to these rules, and one draw needn't show every extreme that they name: `slot_counts`: slots at and beyond the count are padding.
All inputs are finite; a program needn't handle non-finite values.
Results may differ from a plain program's by a relative error of at most 0.0003.
Values sent between devices are 32-bit elements; how exact they have to be, the bound alone decides.
A program may use at most 128 MiB of HBM per device.

v0:
```python
import functools

import jax
import jax.numpy as jnp
from jax import lax
from jax.experimental import pallas as pl
from jax.experimental.pallas import tpu as pltpu
from jax.sharding import PartitionSpec as P

TAU = 0.15
KAPPA = 1.0
MESH = pl.DeviceIdType.MESH
VMEM = pl.BlockSpec(memory_space=pltpu.VMEM)
SMEM = pl.BlockSpec(memory_space=pltpu.SMEM)
F32 = jnp.float32
BF16 = jnp.bfloat16
LANES = 128
ELEM = 8


def log2(n):
    assert n & (n - 1) == 0
    return n.bit_length() - 1


def iota(shape, dim):
    return lax.broadcasted_iota(jnp.int32, shape, dim)


def split(x, terms):
    parts = []
    for _ in range(terms):
        part = x.astype(BF16)
        parts.append(part)
        x = x - part.astype(F32)
    return parts


def hot(rows, index):
    return jnp.where(iota((rows, index.shape[1]), 0) == index, 1.0, 0.0).astype(BF16)


def place():
    return lax.axis_index("group"), lax.axis_index("dev")


def greet(offsets, sizes):
    barrier = pltpu.get_barrier_semaphore()
    me = place()
    for off in offsets:
        target = tuple(lax.rem(m + o, n) for m, o, n in zip(me, off, sizes))
        pl.semaphore_signal(barrier, inc=1, device_id=target, device_id_type=MESH)
    pl.semaphore_wait(barrier, len(offsets))


def all_offsets(sizes):
    return [(a, b) for a in range(sizes[0]) for b in range(sizes[1]) if (a, b) != (0, 0)]


def dev_offsets(sizes):
    return [(0, b) for b in range(1, sizes[1])]


def send(src, dst, send_sem, recv_sem, target):
    return pltpu.make_async_remote_copy(
        src_ref=src, dst_ref=dst, send_sem=send_sem, recv_sem=recv_sem,
        device_id=target, device_id_type=MESH,
    )


def shifted(me, off, sizes):
    return tuple(lax.rem(m + o, n) for m, o, n in zip(me, off, sizes))


def spread_rows(rows_ref, out_ref, sizes, send_sem, recv_sem):
    me = place()
    copies = []
    for off in all_offsets(sizes):
        slot = off[0] * sizes[1] + off[1]
        target = shifted(me, off, sizes)
        copy = send(rows_ref.at[target[1]], out_ref.at[slot], send_sem.at[slot], recv_sem.at[slot], target)
        copy.start()
        copies.append(copy)
    out_ref[0] = rows_ref[me[1]]
    return copies


def halo_copies(edge_ref, halo_ref, sizes, send_sem, recv_sem, act):
    g, s = place()
    count = sizes[1]
    up = send(edge_ref.at[1], halo_ref.at[0], send_sem.at[0], recv_sem.at[0], (g, lax.rem(s + 1, count)))
    down = send(edge_ref.at[0], halo_ref.at[1], send_sem.at[1], recv_sem.at[1], (g, lax.rem(s + count - 1, count)))
    has_up = s < count - 1
    has_down = s > 0
    if act == "start":
        pl.when(has_up)(up.start)
        pl.when(has_down)(down.start)
    else:
        pl.when(has_up)(up.wait_send)
        pl.when(has_down)(down.wait_send)
        pl.when(has_down)(up.wait_recv)
        pl.when(has_up)(down.wait_recv)


def blank_ends(halo_ref, sizes):
    g, s = place()

    @pl.when(s == 0)
    def _():
        halo_ref[0] = jnp.zeros(halo_ref.shape[1:], F32)

    @pl.when(s == sizes[1] - 1)
    def _():
        halo_ref[1] = jnp.zeros(halo_ref.shape[1:], F32)


def index_kernel(sizes, nodes_ref, state_ref, table_ref, halo_ref, rows, edge, ss, rs, hs, hr):
    width = state_ref.shape[3]
    for p in range(sizes[1]):
        rows[p] = nodes_ref[0, 0, p : p + 1, :]
    edge[0] = state_ref[0, :, :, 0:1, :]
    edge[1] = state_ref[0, :, :, width - 1 : width, :]
    greet(all_offsets(sizes), sizes)
    copies = spread_rows(rows, table_ref, sizes, ss, rs)
    halo_copies(edge, halo_ref, sizes, hs, hr, "start")
    blank_ends(halo_ref, sizes)
    for copy in copies:
        copy.wait()
    halo_copies(edge, halo_ref, sizes, hs, hr, "wait")


def pick_kernel(sizes, disp_ref, table_ref, out_ref, flat, picked, ss, rs):
    count = sizes[1]
    highs = disp_ref.shape[1] // LANES
    for c in range(3):
        for h in range(highs):
            flat[c * highs + h : c * highs + h + 1, :] = disp_ref[c : c + 1, h * LANES : (h + 1) * LANES]
    left = jnp.concatenate(split(flat[...], 3), axis=1)
    shift = log2(LANES)
    for b in range(count):
        node = table_ref[b]
        low = hot(LANES, node & (LANES - 1))
        got = jnp.dot(left, jnp.concatenate([low] * 3, axis=0), preferred_element_type=F32)
        mask = iota((highs, LANES), 0) == (node >> shift)
        for c in range(3):
            part = jnp.where(mask, got[c * highs : (c + 1) * highs, :], 0.0)
            picked[b, c : c + 1, :] = jnp.sum(part, axis=0, keepdims=True)
    offsets = dev_offsets(sizes)
    greet(offsets, sizes)
    me = place()
    copies = []
    for off in offsets:
        b = off[1]
        target = shifted(me, (0, count - b), sizes)
        copy = send(picked.at[b], out_ref.at[b], ss.at[b], rs.at[b], target)
        copy.start()
        copies.append(copy)
    out_ref[0] = picked[0]
    for copy in copies:
        copy.wait()


def live_rows(counts_ref, p, capacity):
    g, _ = place()
    top = jnp.where(g < lax.axis_size("group") - 1, counts_ref[0, 0, p], 0)
    return jnp.where(iota((1, capacity), 1) < top, 1.0, 0.0)


def sweep(q_ref, halo_ref, forcing_ref, coupling_ref, out_ref, out_lead, q_lead):
    comps, depth, width, span = q_ref.shape[-4:]

    def body(z, carry):
        lane = iota((width, span), 1)
        sub = iota((width, span), 0)
        low_z = jnp.where(z > 0, 1.0, 0.0)
        high_z = jnp.where(z < depth - 1, 1.0, 0.0)
        centers = [q_ref[(*q_lead, a, z)] for a in range(comps)]
        for a in range(comps):
            c = centers[a]
            near = q_ref[(*q_lead, a, jnp.maximum(z - 1, 0))] * low_z
            near = near + q_ref[(*q_lead, a, jnp.minimum(z + 1, depth - 1))] * high_z
            near = near + jnp.where(sub == 0, halo_ref[0, a, z], pltpu.roll(c, 1, 0))
            near = near + jnp.where(sub == width - 1, halo_ref[1, a, z], pltpu.roll(c, width - 1, 0))
            near = near + jnp.where(lane == 0, 0.0, pltpu.roll(c, 1, 1))
            near = near + jnp.where(lane == span - 1, 0.0, pltpu.roll(c, span - 1, 1))
            mixed = near - 6.0 * c
            for b in range(comps):
                mixed = mixed + coupling_ref[a, b] * centers[b]
            if a < 3:
                mixed = mixed + forcing_ref[z, :, a * span : (a + 1) * span]
            out_ref[(*out_lead, a, z)] = c + TAU * mixed
        return carry

    lax.fori_loop(0, depth, body, 0)


def spread_kernel(
    count, arrived_ref, counts_ref, cells_ref, weights_ref, state_ref, halo_ref, coupling_ref,
    forcing_ref, first_ref, edge_ref, total, masked,
):
    depth, width, span = state_ref.shape[-3:]
    capacity = arrived_ref.shape[2]
    row_count = depth * width
    shift = log2(span)
    _, s = place()
    for p in range(count):
        masked[p] = arrived_ref[lax.rem(p - s + count, count)] * live_rows(counts_ref, p, capacity)
    total[...] = jnp.zeros(total.shape, F32)

    def corner(j, carry):
        cell = cells_ref[0, 0, j]
        weight = weights_ref[0, 0, j]
        left, high, low = [], [], []
        for p in range(count):
            index = cell[p : p + 1, :]
            left.append(hot(row_count, index >> shift))
            mask = iota((span, capacity), 0) == (index & (span - 1))
            scaled = KAPPA * weight[p : p + 1, :] * masked[p]
            parts = split(scaled, 2)
            for into, part in zip((high, low), parts):
                part = part.astype(F32)
                into.append(
                    jnp.concatenate(
                        [jnp.where(mask, part[c : c + 1, :], 0.0).astype(BF16) for c in range(3)], axis=0
                    )
                )
        left = jnp.concatenate(left, axis=1)
        for right in (high, low):
            total[...] += lax.dot_general(
                left, jnp.concatenate(right, axis=1), (((1,), (1,)), ((), ())), preferred_element_type=F32
            )
        return carry

    lax.fori_loop(0, cells_ref.shape[2], corner, 0)
    forcing_ref[...] = total[...].reshape(depth, width, 3 * span)
    sweep(state_ref, halo_ref, forcing_ref, coupling_ref, first_ref, (), (0,))
    edge_ref[0] = first_ref[:, :, 0:1, :]
    edge_ref[1] = first_ref[:, :, width - 1 : width, :]


def halo_kernel(sizes, edge_ref, halo_ref, hs, hr):
    greet([(0, 1), (0, sizes[1] - 1)], sizes)
    halo_copies(edge_ref, halo_ref, sizes, hs, hr, "start")
    blank_ends(halo_ref, sizes)
    halo_copies(edge_ref, halo_ref, sizes, hs, hr, "wait")


def sample_kernel(
    count, first_ref, halo_ref, forcing_ref, coupling_ref, state_ref, cells_ref, weights_ref, counts_ref,
    out_ref, force_ref, table,
):
    depth, width, span = state_ref.shape[-3:]
    capacity = cells_ref.shape[-1]
    row_count = depth * width
    shift = log2(span)
    g, _ = place()
    fluid = g < lax.axis_size("group") - 1
    sweep(first_ref, halo_ref, forcing_ref, coupling_ref, out_ref, (0,), ())
    for c in range(3):
        parts = split(out_ref[0, c].reshape(row_count, span).T, 2)
        for t, part in enumerate(parts):
            table[c * span : (c + 1) * span, t * row_count : (t + 1) * row_count] = part

    @pl.when(jnp.logical_not(fluid))
    def _():
        out_ref[...] = state_ref[...]

    force_ref[...] = jnp.zeros(force_ref.shape, F32)

    def corner(j, carry):
        cell = cells_ref[0, 0, j]
        weight = weights_ref[0, 0, j]
        rows = jnp.concatenate([hot(row_count, cell[p : p + 1, :] >> shift) for p in range(count)], axis=1)
        got = jnp.dot(table[...], jnp.concatenate([rows, rows], axis=0), preferred_element_type=F32)
        for p in range(count):
            mask = iota((span, capacity), 0) == (cell[p : p + 1, :] & (span - 1))
            for c in range(3):
                part = jnp.where(mask, got[c * span : (c + 1) * span, p * capacity : (p + 1) * capacity], 0.0)
                value = jnp.sum(part, axis=0, keepdims=True) * weight[p : p + 1, :]
                force_ref[p, c : c + 1, :] += value
        return carry

    lax.fori_loop(0, cells_ref.shape[2], corner, 0)
    for p in range(count):
        force_ref[p] = force_ref[p] * live_rows(counts_ref, p, capacity)


def force_kernel(sizes, rows_ref, out_ref, ss, rs):
    greet(all_offsets(sizes), sizes)
    for copy in spread_rows(rows_ref, out_ref, sizes, ss, rs):
        copy.wait()


def fold(product):
    total = product[:, :LANES]
    for h in range(1, product.shape[1] // LANES):
        total = total + product[:, h * LANES : (h + 1) * LANES]
    return jnp.sum(total, axis=0, keepdims=True)


def solid_kernel(
    sizes, table_ref, force_ref, flex_ref, disp_ref, prev_ref, hist_ref, solid_ref, gram_ref, total, nodal, partial
):
    groups, count = sizes
    g, _ = place()
    capacity = table_ref.shape[2]
    n_local = disp_ref.shape[1]
    blocks = n_local // ELEM
    wide = blocks // LANES
    elem_shift, lane_shift = log2(ELEM), log2(LANES)
    total[...] = jnp.zeros(total.shape, F32)

    def source_group(gs, carry):
        base = lax.rem(g - gs + groups, groups) * count
        left, high, low = [], [], []
        for b in range(count):
            node = table_ref[base + b]
            block = node >> elem_shift
            row = (block >> lane_shift) * ELEM + (node & (ELEM - 1))
            left.append(hot(wide * ELEM, row))
            mask = iota((LANES, capacity), 0) == (block & (LANES - 1))
            for into, part in zip((high, low), split(force_ref[base + b], 2)):
                part = part.astype(F32)
                into.append(
                    jnp.concatenate(
                        [jnp.where(mask, part[c : c + 1, :], 0.0).astype(BF16) for c in range(3)], axis=0
                    )
                )
        left = jnp.concatenate(left, axis=1)
        for right in (high, low):
            total[...] += lax.dot_general(
                left, jnp.concatenate(right, axis=1), (((1,), (1,)), ((), ())), preferred_element_type=F32
            )
        return carry

    lax.fori_loop(0, groups - 1, source_group, 0)
    u = jnp.concatenate(
        [
            jnp.concatenate(
                [total[h * ELEM : (h + 1) * ELEM, c * LANES : (c + 1) * LANES] for h in range(wide)], axis=1
            )
            for c in range(3)
        ],
        axis=0,
    )
    for o in range(3 * ELEM):
        nodal[o : o + 1, :] = jnp.sum(flex_ref[o] * u, axis=0, keepdims=True)

    per_row = LANES // ELEM
    own = iota((ELEM, LANES), 0) == (iota((ELEM, LANES), 1) >> log2(per_row))
    lines = []
    for c in range(3):
        for h in range(wide):
            lines.append(
                jnp.concatenate(
                    [
                        jnp.where(own, nodal[c * ELEM + i : c * ELEM + i + 1, h * LANES : (h + 1) * LANES], 0.0)
                        for i in range(ELEM)
                    ],
                    axis=1,
                )
            )
    lines = jnp.concatenate(lines, axis=0)
    k = iota((ELEM * LANES, LANES), 0)
    move = (k & (per_row - 1)) * ELEM + (k >> lane_shift)
    move = jnp.where(move == iota((ELEM * LANES, LANES), 1), 1.0, 0.0).astype(BF16)
    solid = 0.0
    for part in reversed(split(lines, 3)):
        solid = solid + jnp.dot(part, move, preferred_element_type=F32)
    per_comp = n_local // LANES
    for c in range(3):
        for h in range(per_comp):
            solid_ref[c : c + 1, h * LANES : (h + 1) * LANES] = solid[c * per_comp + h : c * per_comp + h + 1, :]

    hist = hist_ref.shape[0]
    order = hist + 1
    residual = solid_ref[...] - disp_ref[...]
    change = residual - prev_ref[...]
    rows = [change] + [hist_ref[h] for h in range(hist)]
    for r in range(order):
        for col in range(r, order):
            value = fold(rows[r] * rows[col])
            partial[col, r : r + 1, :] = value
            if col != r:
                partial[r, col : col + 1, :] = value
        partial[order, r : r + 1, :] = fold(rows[r] * residual)
    lane = iota((order, LANES), 1)
    gram = jnp.zeros((order, LANES), F32)
    for col in range(order + 1):
        gram = gram + jnp.where(lane == col, jnp.sum(partial[col], axis=1, keepdims=True), 0.0)
    gram_ref[...] = gram


def update_kernel(sizes, gram_ref, solid_ref, prev_ref, hist_ref, out_ref, parts, ss, rs):
    offsets = dev_offsets(sizes)
    greet(offsets, sizes)
    me = place()
    copies = []
    for off in offsets:
        b = off[1]
        copy = send(gram_ref, parts.at[b], ss.at[b], rs.at[b], shifted(me, off, sizes))
        copy.start()
        copies.append(copy)
    for copy in copies:
        copy.wait()
    order = gram_ref.shape[0]
    m = jnp.zeros(gram_ref.shape, F32)
    parts[0] = gram_ref[...]
    for owner in range(sizes[1]):
        m = m + parts[lax.rem(me[1] - owner + sizes[1], sizes[1])]
    sub = iota(m.shape, 0)
    for k in range(order):
        row = m[k : k + 1, :] / m[k : k + 1, k : k + 1]
        m = jnp.where(sub == k, row, m - m[:, k : k + 1] * row)
    solid = solid_ref[...]
    result = solid - m[0:1, order : order + 1] * (solid - prev_ref[...])
    for h in range(order - 1):
        result = result - m[h + 1 : h + 2, order : order + 1] * hist_ref[h]
    out_ref[...] = result


def call(kernel, outs, ins, scratch=(), collective=None, side=False):
    return pl.pallas_call(
        kernel,
        out_shape=tuple(jax.ShapeDtypeStruct(*o) for o in outs),
        in_specs=list(ins),
        out_specs=tuple(VMEM for _ in outs),
        scratch_shapes=list(scratch),
        compiler_params=pltpu.CompilerParams(
            collective_id=collective, has_side_effects=side, vmem_limit_bytes=48 * 1024 * 1024
        ),
    )


def per_device(
    sizes, fluid_state, coupling, displacement, slot_cells, slot_weights, slot_nodes, slot_counts,
    flexibility, resid_prev, struct_prev, v_hist, w_hist,
):
    groups, count = sizes
    total = groups * count
    comps, depth, width, span = fluid_state.shape[1:]
    capacity = slot_nodes.shape[-1]
    n_local = displacement.shape[1]
    order = v_hist.shape[0] + 1
    dma = pltpu.SemaphoreType.DMA
    halo = (2, comps, depth, 1, span)
    table, halo_zero = call(
        functools.partial(index_kernel, sizes),
        [((total, 1, capacity), jnp.int32), (halo, F32)],
        [VMEM, VMEM],
        [
            pltpu.VMEM((count, 1, capacity), jnp.int32), pltpu.VMEM(halo, F32),
            dma((total,)), dma((total,)), dma((2,)), dma((2,)),
        ],
        0, True,
    )(slot_nodes, fluid_state)
    (arrived,) = call(
        functools.partial(pick_kernel, sizes),
        [((count, 3, capacity), F32)],
        [VMEM, VMEM],
        [
            pltpu.VMEM((3 * n_local // LANES, LANES), F32), pltpu.VMEM((count, 3, capacity), F32),
            dma((count,)), dma((count,)),
        ],
        1, True,
    )(displacement, table)
    forcing, first, edge = call(
        functools.partial(spread_kernel, count),
        [((depth, width, 3 * span), F32), ((comps, depth, width, span), F32), (halo, F32)],
        [VMEM, SMEM, VMEM, VMEM, VMEM, VMEM, SMEM],
        [pltpu.VMEM((depth * width, 3 * span), F32), pltpu.VMEM((count, 3, capacity), F32)],
    )(arrived, slot_counts, slot_cells, slot_weights, fluid_state, halo_zero, coupling)
    (halo_one,) = call(
        functools.partial(halo_kernel, sizes), [(halo, F32)], [VMEM], [dma((2,)), dma((2,))], 2, True
    )(edge)
    fluid_out, force = call(
        functools.partial(sample_kernel, count),
        [(fluid_state.shape, F32), ((count, 3, capacity), F32)],
        [VMEM, VMEM, VMEM, SMEM, VMEM, VMEM, VMEM, SMEM],
        [pltpu.VMEM((3 * span, 2 * depth * width), BF16)],
    )(first, halo_one, forcing, coupling, fluid_state, slot_cells, slot_weights, slot_counts)
    (forces,) = call(
        functools.partial(force_kernel, sizes),
        [((total, 3, capacity), F32)], [VMEM], [dma((total,)), dma((total,))], 3, True,
    )(force)
    solid, gram = call(
        functools.partial(solid_kernel, sizes),
        [((3, n_local), F32), ((order, LANES), F32)],
        [VMEM] * 6,
        [
            pltpu.VMEM((n_local // LANES, 3 * LANES), F32), pltpu.VMEM((3 * ELEM, n_local // ELEM), F32),
            pltpu.VMEM((order + 1, order, LANES), F32),
        ],
    )(table, forces, flexibility, displacement, resid_prev, v_hist)
    (updated,) = call(
        functools.partial(update_kernel, sizes),
        [((3, n_local), F32)],
        [VMEM] * 4,
        [pltpu.VMEM((count, order, LANES), F32), dma((count,)), dma((count,))],
        4, True,
    )(gram, solid, struct_prev, w_hist)
    return fluid_out, updated


def solution(mesh):
    sizes = (mesh.shape["group"], mesh.shape["dev"])
    return jax.shard_map(
        functools.partial(per_device, sizes),
        mesh=mesh,
        in_specs=(
            P("group", None, None, "dev", None),
            P(),
            P(None, "dev"),
            P("group", "dev", None, None, None),
            P("group", "dev", None, None, None),
            P("group", "dev", None, None),
            P("group", "dev", None),
            P(None, None, "dev"),
            P(None, "dev"),
            P(None, "dev"),
            P(None, None, "dev"),
            P(None, None, "dev"),
        ),
        out_specs=(P("group", None, None, "dev", None), P(None, "dev")),
        check_vma=False,
    )
```

profile of v0, /device:TPU:0, one launch (start us, length us, event | category | flops | bytes accessed | tf_op | source)
XLA Modules:
  0.0 63.6 jit_solution(12655339659913264634)
XLA Ops:
  0.6 0.0 copy-start
  0.6 1.0 %copy-done = f32[1,4,16,16,128]{4,3,2,1,0:T(8,128)S(1)} copy-done((f32[1,4,16,16,128]{4,3,2,1,0:T(8,128)S(1)}, f32[1,4,16,16,128]{4,3,2,1,0:T(8,128)}, u32[]{:S(2)}) %copy-start) | copy-done | bytes 524312
  1.7 0.0 copy-start.14
  1.7 0.7 %copy-done.14 = s32[1,1,8,128]{3,2,1,0:T(8,128)S(1)} copy-done((s32[1,1,8,128]{3,2,1,0:T(8,128)S(1)}, s32[1,1,8,128]{3,2,1,0:T(8,128)}, u32[]{:S(2)}) %copy-start.14) | copy-done | bytes 4120
  2.4 0.0 copy-start.2
  2.4 0.0 copy-start.13
  2.4 0.0 copy-start.16
  2.4 10.1 %shard_map.131 = (s32[32,1,128]{2,1,0:T(1,128)S(1)}, f32[2,4,16,1,128]{4,3,2,1,0:T(1,128)S(1)}) custom-call(s32[1,1,8,128]{3,2,1,0:T(8,128)S(1)} %copy-done.14, f32[1,4,16,16,128]{4,3,2,1,0:T(8,128)S(1)} %copy-done), custom_call_target="tpu_custom_call" | custom-call | tf_op jit(solution)/shard_map/pallas_call | solution.py:447
  12.5 0.0 copy-start.4
  12.5 0.8 %copy-done.4 = f32[3,4096]{1,0:T(4,128)S(1)} copy-done((f32[3,4096]{1,0:T(4,128)S(1)}, f32[3,4096]{1,0:T(4,128)}, u32[]{:S(2)}) %copy-start.4) | copy-done | bytes 49176
  13.3 6.0 %shard_map.132.arrived_ref = f32[8,3,128]{2,1,0:T(4,128)S(1)} custom-call(f32[3,4096]{1,0:T(4,128)S(1)} %copy-done.4, s32[32,1,128]{2,1,0:T(1,128)S(1)} %get-tuple-element.11.table_ref), custom_call_target="tpu_custom_call" | custom-call | tf_op jit(solution)/shard_map/pallas_call | solution.py:457
  19.3 0.0 copy-start.1
  19.3 1.0 %copy-done.1 = f32[1,4,16,16,128]{4,3,2,1,0:T(8,128)S(1)} copy-done((f32[1,4,16,16,128]{4,3,2,1,0:T(8,128)S(1)}, f32[1,4,16,16,128]{4,3,2,1,0:T(8,128)}, u32[]{:S(2)}) %copy-start.1) | copy-done | bytes 524312
  20.4 0.0 copy-start.6
  20.4 0.8 %copy-done.6 = s32[1,1,8,8,128]{4,3,2,1,0:T(8,128)S(1)} copy-done((s32[1,1,8,8,128]{4,3,2,1,0:T(8,128)S(1)}, s32[1,1,8,8,128]{4,3,2,1,0:T(8,128)}, u32[]{:S(2)}) %copy-start.6) | copy-done | bytes 32792
  21.1 0.0 copy-start.8
  21.1 0.8 %copy-done.8 = f32[1,1,8,8,128]{4,3,2,1,0:T(8,128)S(1)} copy-done((f32[1,1,8,8,128]{4,3,2,1,0:T(8,128)S(1)}, f32[1,1,8,8,128]{4,3,2,1,0:T(8,128)}, u32[]{:S(2)}) %copy-start.8) | copy-done | bytes 32792
  21.9 0.0 copy-start.12
  21.9 0.7 %copy-done.12 = f32[4,4]{1,0:T(4,128)S(1)} copy-done((f32[4,4]{1,0:T(4,128)S(1)}, f32[4,4]{1,0:T(4,128)}, u32[]{:S(2)}) %copy-start.12) | copy-done | bytes 88
  22.6 0.0 copy-start.15
  22.6 0.7 %copy-done.15 = s32[1,1,8]{2,1,0:T(1,128)S(1)} copy-done((s32[1,1,8]{2,1,0:T(1,128)S(1)}, s32[1,1,8]{2,1,0:T(1,128)}, u32[]{:S(2)}) %copy-start.15) | copy-done | bytes 56
  23.2 0.0 copy-start.17
  23.2 8.1 %shard_map.133 = (f32[16,16,384]{2,1,0:T(8,128)S(1)}, f32[4,16,16,128]{3,2,1,0:T(8,128)S(1)}, f32[2,4,16,1,128]{4,3,2,1,0:T(1,128)S(1)}) custom-call(f32[8,3,128]{2,1,0:T(4,128)S(1)} %shard_map.132.arrived_ref, s32[1,1,8]{2,1,0:T(1,128)S(1)} %copy-done.15, s32[1,1,8,8,128]{4,3,2,1,0:T(8,128)S(1)} %copy-done.6, f32[1,1,8,8,128]{4,3,2,1,0:T(8,128)S(1)} %copy-done.8, ...), custom_call_target="tpu_custom_call" | custom-call | tf_op jit(solution)/shard_map/pallas_call | solution.py:467
  31.3 3.5 %shard_map.134.halo_ref = f32[2,4,16,1,128]{4,3,2,1,0:T(1,128)S(1)} custom-call(f32[2,4,16,1,128]{4,3,2,1,0:T(1,128)S(1)} %get-tuple-element.14.edge_ref), custom_call_target="tpu_custom_call" | custom-call | tf_op jit(solution)/shard_map/pallas_call | solution.py:473
  34.8 0.0 copy-done.2
  34.8 0.0 copy-done.13
  34.8 0.0 copy-done.16
  34.8 0.0 copy-start.7
  34.9 0.7 %copy-done.7 = s32[1,1,8,8,128]{4,3,2,1,0:T(8,128)S(1)} copy-done((s32[1,1,8,8,128]{4,3,2,1,0:T(8,128)S(1)}, s32[1,1,8,8,128]{4,3,2,1,0:T(8,128)}, u32[]{:S(2)}) %copy-start.7) | copy-done | bytes 32792
  35.6 0.0 copy-start.9
  35.6 0.8 %copy-done.9 = f32[1,1,8,8,128]{4,3,2,1,0:T(8,128)S(1)} copy-done((f32[1,1,8,8,128]{4,3,2,1,0:T(8,128)S(1)}, f32[1,1,8,8,128]{4,3,2,1,0:T(8,128)}, u32[]{:S(2)}) %copy-start.9) | copy-done | bytes 32792
  36.4 0.0 copy-start.3
  36.4 0.0 copy-start.5
  36.4 0.0 copy-start.10
  36.4 8.4 %shard_map.135 = (f32[1,4,16,16,128]{4,3,2,1,0:T(8,128)}, f32[8,3,128]{2,1,0:T(4,128)S(1)}) custom-call(f32[4,16,16,128]{3,2,1,0:T(8,128)S(1)} %get-tuple-element.13.first_ref, f32[2,4,16,1,128]{4,3,2,1,0:T(1,128)S(1)} %shard_map.134.halo_ref, f32[16,16,384]{2,1,0:T(8,128)S(1)} %get-tuple-element.15.forcing_ref, f32[4,4]{1,0:T(4,128)S(1)} %copy-done.13, ...), custom_call_target="tpu_custom_call" | custom-call | tf_op jit(solution)/shard_map/pallas_call | solution.py:476
  44.8 8.2 %shard_map.136.force_ref = f32[32,3,128]{2,1,0:T(4,128)S(1)} custom-call(f32[8,3,128]{2,1,0:T(4,128)S(1)} %get-tuple-element.17.rows_ref), custom_call_target="tpu_custom_call" | custom-call | tf_op jit(solution)/shard_map/pallas_call | solution.py:482
  53.0 0.0 copy-done.17
  53.0 0.0 copy-start.18
  53.0 0.2 copy.14.hist_ref
  53.2 0.0 copy-done.3
  53.3 0.0 copy-done.5
  53.3 0.0 copy-done.10
  53.3 0.0 copy-start.11
  53.3 3.0 %shard_map.137 = (f32[3,4096]{1,0:T(4,128)S(1)}, f32[8,128]{1,0:T(8,128)S(1)}) custom-call(s32[32,1,128]{2,1,0:T(1,128)S(1)} %get-tuple-element.11.table_ref, f32[32,3,128]{2,1,0:T(4,128)S(1)} %shard_map.136.force_ref, f32[24,24,512]{2,1,0:T(8,128)S(1)} %copy-done.3, f32[3,4096]{1,0:T(4,128)S(1)} %copy-done.5, f32[3,4096]{1,0:T(4,128)S(1)} %copy-done.10, ...), custom_call_target="tpu_custom_call" | custom-call | tf_op jit(solution)/shard_map/pallas_call | solution.py:486
  56.3 0.0 copy-done.18
  56.3 0.2 copy.15.hist_ref
  56.5 0.0 copy-done.11
  56.5 6.4 %shard_map.138 = f32[3,4096]{1,0:T(4,128)S(1)} custom-call(f32[8,128]{1,0:T(8,128)S(1)} %get-tuple-element.18.gram_ref, f32[3,4096]{1,0:T(4,128)S(1)} %get-tuple-element.19.solid_ref, f32[3,4096]{1,0:T(4,128)S(1)} %copy-done.11, f32[7,3,4096]{2,1,0:T(4,128)S(1)} %copy.15.hist_ref), custom_call_target="tpu_custom_call" | custom-call | tf_op jit(solution)/shard_map/pallas_call | solution.py:495
  63.0 0.6 copy.17
Async XLA Ops:
  0.6 1.0 %copy-start = (f32[1,4,16,16,128]{4,3,2,1,0:T(8,128)S(1)}, f32[1,4,16,16,128]{4,3,2,1,0:T(8,128)}, u32[]{:S(2)}) copy-start(f32[1,4,16,16,128]{4,3,2,1,0:T(8,128)} %state_ref.5) | copy-start | bytes 1572868
  1.7 0.7 %copy-start.14 = (s32[1,1,8,128]{3,2,1,0:T(8,128)S(1)}, s32[1,1,8,128]{3,2,1,0:T(8,128)}, u32[]{:S(2)}) copy-start(s32[1,1,8,128]{3,2,1,0:T(8,128)} %nodes_ref.1) | copy-start | bytes 12292
  2.4 32.5 %copy-start.2 = (f32[1,4,16,16,128]{4,3,2,1,0:T(8,128)S(1)}, f32[1,4,16,16,128]{4,3,2,1,0:T(8,128)}, u32[]{:S(2)}) copy-start(f32[1,4,16,16,128]{4,3,2,1,0:T(8,128)} %state_ref.5) | copy-start | bytes 1572868
  2.4 32.5 %copy-start.13 = (f32[4,4]{1,0:T(4,128)S(1)}, f32[4,4]{1,0:T(4,128)}, u32[]{:S(2)}) copy-start(f32[4,4]{1,0:T(4,128)} %coupling_ref.3) | copy-start | bytes 196
  2.4 32.5 %copy-start.16 = (s32[1,1,8]{2,1,0:T(1,128)S(1)}, s32[1,1,8]{2,1,0:T(1,128)}, u32[]{:S(2)}) copy-start(s32[1,1,8]{2,1,0:T(1,128)} %counts_ref.3) | copy-start | bytes 100
  12.5 0.8 %copy-start.4 = (f32[3,4096]{1,0:T(4,128)S(1)}, f32[3,4096]{1,0:T(4,128)}, u32[]{:S(2)}) copy-start(f32[3,4096]{1,0:T(4,128)} %disp_ref.3) | copy-start | bytes 147460
  19.3 1.0 %copy-start.1 = (f32[1,4,16,16,128]{4,3,2,1,0:T(8,128)S(1)}, f32[1,4,16,16,128]{4,3,2,1,0:T(8,128)}, u32[]{:S(2)}) copy-start(f32[1,4,16,16,128]{4,3,2,1,0:T(8,128)} %state_ref.5) | copy-start | bytes 1572868
  20.4 0.8 %copy-start.6 = (s32[1,1,8,8,128]{4,3,2,1,0:T(8,128)S(1)}, s32[1,1,8,8,128]{4,3,2,1,0:T(8,128)}, u32[]{:S(2)}) copy-start(s32[1,1,8,8,128]{4,3,2,1,0:T(8,128)} %cells_ref.3) | copy-start | bytes 98308
  21.1 0.8 %copy-start.8 = (f32[1,1,8,8,128]{4,3,2,1,0:T(8,128)S(1)}, f32[1,1,8,8,128]{4,3,2,1,0:T(8,128)}, u32[]{:S(2)}) copy-start(f32[1,1,8,8,128]{4,3,2,1,0:T(8,128)} %weights_ref.3) | copy-start | bytes 98308
  21.9 0.7 %copy-start.12 = (f32[4,4]{1,0:T(4,128)S(1)}, f32[4,4]{1,0:T(4,128)}, u32[]{:S(2)}) copy-start(f32[4,4]{1,0:T(4,128)} %coupling_ref.3) | copy-start | bytes 196
  22.6 0.7 %copy-start.15 = (s32[1,1,8]{2,1,0:T(1,128)S(1)}, s32[1,1,8]{2,1,0:T(1,128)}, u32[]{:S(2)}) copy-start(s32[1,1,8]{2,1,0:T(1,128)} %counts_ref.3) | copy-start | bytes 100
  23.2 29.8 %copy-start.17 = (f32[7,3,4096]{2,0,1:T(8,128)S(1)}, f32[7,3,4096]{2,0,1:T(8,128)}, u32[]{:S(2)}) copy-start(f32[7,3,4096]{2,0,1:T(8,128)} %param.22) | copy-start | bytes 1032196
  34.8 0.8 %copy-start.7 = (s32[1,1,8,8,128]{4,3,2,1,0:T(8,128)S(1)}, s32[1,1,8,8,128]{4,3,2,1,0:T(8,128)}, u32[]{:S(2)}) copy-start(s32[1,1,8,8,128]{4,3,2,1,0:T(8,128)} %cells_ref.3) | copy-start | bytes 98308
  35.6 0.8 %copy-start.9 = (f32[1,1,8,8,128]{4,3,2,1,0:T(8,128)S(1)}, f32[1,1,8,8,128]{4,3,2,1,0:T(8,128)}, u32[]{:S(2)}) copy-start(f32[1,1,8,8,128]{4,3,2,1,0:T(8,128)} %weights_ref.3) | copy-start | bytes 98308
  36.4 16.9 %copy-start.3 = (f32[24,24,512]{2,1,0:T(8,128)S(1)}, f32[24,24,512]{2,1,0:T(8,128)}, u32[]{:S(2)}) copy-start(f32[24,24,512]{2,1,0:T(8,128)} %flex_ref.1) | copy-start | bytes 3538948
  36.4 16.9 %copy-start.5 = (f32[3,4096]{1,0:T(4,128)S(1)}, f32[3,4096]{1,0:T(4,128)}, u32[]{:S(2)}) copy-start(f32[3,4096]{1,0:T(4,128)} %disp_ref.3) | copy-start | bytes 147460
  36.4 16.9 %copy-start.10 = (f32[3,4096]{1,0:T(4,128)S(1)}, f32[3,4096]{1,0:T(4,128)}, u32[]{:S(2)}) copy-start(f32[3,4096]{1,0:T(4,128)} %prev_ref.2) | copy-start | bytes 147460
  53.0 3.3 %copy-start.18 = (f32[7,3,4096]{2,0,1:T(8,128)S(1)}, f32[7,3,4096]{2,0,1:T(8,128)}, u32[]{:S(2)}) copy-start(f32[7,3,4096]{2,0,1:T(8,128)} %param.23) | copy-start | bytes 1032196
  53.3 3.2 %copy-start.11 = (f32[3,4096]{1,0:T(4,128)S(1)}, f32[3,4096]{1,0:T(4,128)}, u32[]{:S(2)}) copy-start(f32[3,4096]{1,0:T(4,128)} %prev_ref.3) | copy-start | bytes 147460
where the time goes:
time: 64.2 us; the launch traced here: 63.6 us
  Pallas kernels  53.7 us (84%)
  local copies, waits for them, and re-layouts  9.1 us (14%)
  between operations  0.82 us (1%)
    pallas_call x1, Pallas kernels, per_device(): call(functools.partial(index_kernel, sizes), [((total, 1, capacity), jnp....  10.1 us
    unnamed x41, local copies, waits for them, and re-layouts  9.1 us
    pallas_call x1, Pallas kernels, per_device(): call(functools.partial(sample_kernel, count), [(fluid_state.shape, F32),...  8.44 us
    pallas_call x1, Pallas kernels, per_device(): call(functools.partial(force_kernel, sizes), [((total, 3, capacity), F32)...  8.16 us
    pallas_call x1, Pallas kernels, per_device(): call(functools.partial(spread_kernel, count), [((depth, width, 3 * span),...  8.1 us
    pallas_call x1, Pallas kernels, per_device(): call(functools.partial(update_kernel, sizes), [((3, n_local), F32)], [VME...  6.43 us
    pallas_call x1, Pallas kernels, per_device(): call(functools.partial(pick_kernel, sizes), [((count, 3, capacity), F32)]...  5.99 us
    pallas_call x1, Pallas kernels, per_device(): call(functools.partial(halo_kernel, sizes), [(halo, F32)], [VMEM], [dma((...  3.47 us

commit v1 on v0

v1 whole, which is shorter than its diff:
```python
import functools

import jax
import jax.numpy as jnp
from jax import lax
from jax.experimental import pallas as pl
from jax.experimental.pallas import tpu as pltpu
from jax.sharding import PartitionSpec as P

TAU = 0.15
KAPPA = 1.0
MESH = pl.DeviceIdType.MESH
F32 = jnp.float32
BF16 = jnp.bfloat16
LANES = 128
ELEM = 8


def log2(n):
    assert n & (n - 1) == 0
    return n.bit_length() - 1


def iota(shape, dim):
    return lax.broadcasted_iota(jnp.int32, shape, dim)


def split(x, terms):
    parts = []
    for _ in range(terms):
        part = x.astype(BF16)
        parts.append(part)
        x = x - part.astype(F32)
    return parts


def hot(rows, index):
    return jnp.where(iota((rows, index.shape[1]), 0) == index, 1.0, 0.0).astype(BF16)


def place():
    return lax.axis_index("group"), lax.axis_index("dev")


def greet(offsets, sizes):
    barrier = pltpu.get_barrier_semaphore()
    me = place()
    for off in offsets:
        target = tuple(lax.rem(m + o, n) for m, o, n in zip(me, off, sizes))
        pl.semaphore_signal(barrier, inc=1, device_id=target, device_id_type=MESH)
    pl.semaphore_wait(barrier, len(offsets))


def send(src, dst, send_sem, recv_sem, target):
    return pltpu.make_async_remote_copy(
        src_ref=src, dst_ref=dst, send_sem=send_sem, recv_sem=recv_sem,
        device_id=target, device_id_type=MESH,
    )


def shifted(me, off, sizes):
    return tuple(lax.rem(m + o, n) for m, o, n in zip(me, off, sizes))


def halo_copies(edge_ref, halo_ref, sizes, send_sem, recv_sem, act):
    g, s = place()
    count = sizes[1]
    up = send(edge_ref.at[1], halo_ref.at[0], send_sem.at[0], recv_sem.at[0], (g, lax.rem(s + 1, count)))
    down = send(edge_ref.at[0], halo_ref.at[1], send_sem.at[1], recv_sem.at[1], (g, lax.rem(s + count - 1, count)))
    has_up = s < count - 1
    has_down = s > 0
    if act == "start":
        pl.when(has_up)(up.start)
        pl.when(has_down)(down.start)
    else:
        pl.when(has_up)(up.wait_send)
        pl.when(has_down)(down.wait_send)
        pl.when(has_down)(up.wait_recv)
        pl.when(has_up)(down.wait_recv)


def blank_ends(halo_ref, sizes):
    g, s = place()

    @pl.when(s == 0)
    def _():
        halo_ref[0] = jnp.zeros(halo_ref.shape[1:], F32)

    @pl.when(s == sizes[1] - 1)
    def _():
        halo_ref[1] = jnp.zeros(halo_ref.shape[1:], F32)


def live_rows(counts_ref, p, capacity):
    g, _ = place()
    top = jnp.where(g < lax.axis_size("group") - 1, counts_ref[0, 0, p], 0)
    return jnp.where(iota((1, capacity), 1) < top, 1.0, 0.0)


def sweep(q_ref, q_lead, forcing_ref, coupling_ref, out_ref):
    comps, depth, width, span = q_ref.shape[-4:]

    def body(z, carry):
        lane = iota((width, span), 1)
        sub = iota((width, span), 0)
        low_z = jnp.where(z > 0, 1.0, 0.0)
        high_z = jnp.where(z < depth - 1, 1.0, 0.0)
        centers = [q_ref[(*q_lead, a, z)] for a in range(comps)]
        for a in range(comps):
            c = centers[a]
            near = q_ref[(*q_lead, a, jnp.maximum(z - 1, 0))] * low_z
            near = near + q_ref[(*q_lead, a, jnp.minimum(z + 1, depth - 1))] * high_z
            near = near + jnp.where(sub == 0, 0.0, pltpu.roll(c, 1, 0))
            near = near + jnp.where(sub == width - 1, 0.0, pltpu.roll(c, width - 1, 0))
            near = near + jnp.where(lane == 0, 0.0, pltpu.roll(c, 1, 1))
            near = near + jnp.where(lane == span - 1, 0.0, pltpu.roll(c, span - 1, 1))
            mixed = near - 6.0 * c
            for b in range(comps):
                mixed = mixed + coupling_ref[a, b] * centers[b]
            if a < 3 and forcing_ref is not None:
                mixed = mixed + forcing_ref[pl.ds(pl.multiple_of(z * width, width), width), a * span : (a + 1) * span]
            out_ref[a, z] = c + TAU * mixed
        return carry

    lax.fori_loop(0, depth, body, 0)


def add_halo(field_ref, halo_ref):
    width = field_ref.shape[2]
    field_ref[:, :, 0:1, :] += TAU * halo_ref[0]
    field_ref[:, :, width - 1 : width, :] += TAU * halo_ref[1]


def take_edges(field_ref, lead, edge_ref):
    width = field_ref.shape[-2]
    edge_ref[0] = field_ref[(*lead, slice(None), slice(None), slice(0, 1), slice(None))]
    edge_ref[1] = field_ref[(*lead, slice(None), slice(None), slice(width - 1, width), slice(None))]


def spread_right(mask, values):
    values = values.astype(F32)
    return jnp.concatenate([jnp.where(mask, values[c : c + 1, :], 0.0).astype(BF16) for c in range(3)], axis=0)


def nt(left, right):
    return lax.dot_general(left, right, (((1,), (1,)), ((), ())), preferred_element_type=F32)


def kernel(
    sizes,
    state_h, coupling_h, disp_h, cells_h, weights_h, nodes_h, counts_h, flex_h, rprev_h, sprev_h, vhist_h, whist_h,
    fluid_h, updated_h,
    state, coupling, disp, cells, weights, nodes, counts, flex, rprev, sprev, vhist, whist,
    in_sems, out_sems, dev_send, dev_recv, group_send, group_recv, halo_send, halo_recv,
    rows, table, edges, halos, flat, picked, arrived, masked, forcing, first, second, sampler,
    force, forces, sums, nodal, solid_s, grams, result,
):
    groups, count = sizes
    me = place()
    g, s = me
    depth, width, span = state.shape[-3:]
    capacity = nodes.shape[-1]
    row_count = depth * width
    n_local = disp.shape[1]
    highs = n_local // LANES
    span_shift, lane_shift, elem_shift = log2(span), log2(LANES), log2(ELEM)

    sources = (nodes_h, state_h, disp_h, coupling_h, counts_h, vhist_h, cells_h, weights_h, flex_h, rprev_h, sprev_h, whist_h)
    targets = (nodes, state, disp, coupling, counts, vhist, cells, weights, flex, rprev, sprev, whist)
    loads = [pltpu.make_async_copy(a, b, in_sems.at[k]) for k, (a, b) in enumerate(zip(sources, targets))]
    for load in loads:
        load.start()
    (l_nodes, l_state, l_disp, l_coupling, l_counts, l_vhist, l_cells, l_weights, l_flex, l_rprev, l_sprev, l_whist) = loads

    l_nodes.wait()
    for p in range(count):
        rows[p] = nodes[0, 0, p : p + 1, :]
    greet([(0, b) for b in range(1, count)] + [(a, 0) for a in range(1, groups)], sizes)

    def to_dev(step, src, dst, b, slot):
        return send(src, dst.at[slot], dev_send.at[step, slot], dev_recv.at[step, slot], shifted(me, (0, b), sizes))

    asked = [to_dev(0, rows.at[lax.rem(s + b, count)], table, b, b) for b in range(1, count)]
    for copy in asked:
        copy.start()
    table[0] = rows[s]

    l_state.wait()
    take_edges(state, (0,), edges.at[0])
    halo_copies(edges.at[0], halos.at[0], sizes, halo_send.at[0], halo_recv.at[0], "start")
    blank_ends(halos.at[0], sizes)

    l_disp.wait()
    for c in range(3):
        for h in range(highs):
            flat[c * highs + h : c * highs + h + 1, :] = disp[c : c + 1, h * LANES : (h + 1) * LANES]
    left = jnp.concatenate(split(flat[...], 3), axis=1)
    answers = []
    for b in range(count):
        if b > 0:
            asked[b - 1].wait_recv()
        node = table[b]
        low = hot(LANES, node & (LANES - 1))
        got = jnp.dot(left, jnp.concatenate([low] * 3, axis=0), preferred_element_type=F32)
        mask = iota((highs, capacity), 0) == (node >> lane_shift)
        for c in range(3):
            part = jnp.where(mask, got[c * highs : (c + 1) * highs, :], 0.0)
            picked[b, c : c + 1, :] = jnp.sum(part, axis=0, keepdims=True)
        if b > 0:
            copy = to_dev(1, picked.at[b], arrived, count - b, b)
            copy.start()
            answers.append(copy)
    arrived[0] = picked[0]

    l_coupling.wait()
    l_counts.wait()
    sweep(state, (0,), None, coupling, first)
    halo_copies(edges.at[0], halos.at[0], sizes, halo_send.at[0], halo_recv.at[0], "wait")
    add_halo(first, halos.at[0])

    l_cells.wait()
    l_weights.wait()
    for copy in answers:
        copy.wait_recv()
    for p in range(count):
        masked[p] = arrived[lax.rem(p - s + count, count)] * live_rows(counts, p, capacity)
    forcing[...] = jnp.zeros(forcing.shape, F32)

    def spread_corner(j, carry):
        cell = cells[0, 0, j]
        weight = weights[0, 0, j]
        left, high, low = [], [], []
        for p in range(count):
            index = cell[p : p + 1, :]
            left.append(hot(row_count, index >> span_shift))
            mask = iota((span, capacity), 0) == (index & (span - 1))
            for into, part in zip((high, low), split(KAPPA * weight[p : p + 1, :] * masked[p], 2)):
                into.append(spread_right(mask, part))
        left = jnp.concatenate(left, axis=1)
        both = nt(left, jnp.concatenate(high, axis=1)) + nt(left, jnp.concatenate(low, axis=1))
        forcing[...] += both
        return carry

    lax.fori_loop(0, cells.shape[2], spread_corner, 0)
    for c in range(3):
        first[c] += TAU * forcing[:, c * span : (c + 1) * span].reshape(depth, width, span)
    take_edges(first, (), edges.at[1])
    halo_copies(edges.at[1], halos.at[1], sizes, halo_send.at[1], halo_recv.at[1], "start")
    blank_ends(halos.at[1], sizes)
    sweep(first, (), forcing, coupling, second)

    l_vhist.wait()
    hist = vhist.shape[1]
    lane = iota((hist, LANES), 1)
    early = jnp.zeros((hist, LANES), F32)
    for h in range(hist):
        product = vhist[0] * vhist[0, h : h + 1, :]
        for c in range(1, 3):
            product = product + vhist[c] * vhist[c, h : h + 1, :]
        early = early + jnp.where(lane == h, jnp.sum(product, axis=1, keepdims=True), 0.0)

    halo_copies(edges.at[1], halos.at[1], sizes, halo_send.at[1], halo_recv.at[1], "wait")
    add_halo(second, halos.at[1])
    fluid = g < groups - 1
    store_fluid = pltpu.make_async_copy(second, fluid_h.at[0], out_sems.at[0])
    store_state = pltpu.make_async_copy(state.at[0], fluid_h.at[0], out_sems.at[0])
    pl.when(fluid)(store_fluid.start)
    pl.when(jnp.logical_not(fluid))(store_state.start)

    for c in range(3):
        for t, part in enumerate(split(second[c].reshape(row_count, span).T, 2)):
            sampler[c * span : (c + 1) * span, t * row_count : (t + 1) * row_count] = part
    force[...] = jnp.zeros(force.shape, F32)

    def sample_corner(j, carry):
        cell = cells[0, 0, j]
        weight = weights[0, 0, j]
        here = jnp.concatenate([hot(row_count, cell[p : p + 1, :] >> span_shift) for p in range(count)], axis=1)
        got = jnp.dot(sampler[...], jnp.concatenate([here, here], axis=0), preferred_element_type=F32)
        for p in range(count):
            mask = iota((span, capacity), 0) == (cell[p : p + 1, :] & (span - 1))
            for c in range(3):
                part = jnp.where(mask, got[c * span : (c + 1) * span, p * capacity : (p + 1) * capacity], 0.0)
                value = jnp.sum(part, axis=0, keepdims=True) * weight[p : p + 1, :]
                force[p, c : c + 1, :] += value
        return carry

    lax.fori_loop(0, cells.shape[2], sample_corner, 0)
    for p in range(count):
        force[p] = force[p] * live_rows(counts, p, capacity)
    pushed = [to_dev(2, force.at[lax.rem(s + b, count)], forces, b, b) for b in range(1, count)]
    for copy in pushed:
        copy.start()
    forces[0] = force[s]

    wide = n_local // ELEM // LANES
    for copy in pushed:
        copy.wait_recv()
    left, high, low = [], [], []
    for b in range(count):
        node = table[b]
        block = node >> elem_shift
        left.append(hot(wide * ELEM, (block >> lane_shift) * ELEM + (node & (ELEM - 1))))
        mask = iota((LANES, capacity), 0) == (block & (LANES - 1))
        for into, part in zip((high, low), split(forces[b], 2)):
            into.append(spread_right(mask, part))
    left = jnp.concatenate(left, axis=1)
    sums[0] = nt(left, jnp.concatenate(high, axis=1)) + nt(left, jnp.concatenate(low, axis=1))
    shared = [
        send(sums.at[0], sums.at[a], group_send.at[a], group_recv.at[a], shifted(me, (a, 0), sizes))
        for a in range(1, groups)
    ]
    for copy in shared:
        copy.start()
    l_flex.wait()
    l_rprev.wait()
    l_sprev.wait()
    l_whist.wait()
    for copy in shared:
        copy.wait_recv()
    total = sums[lax.rem(g + groups, groups)]
    for gs in range(1, groups):
        total = total + sums[lax.rem(g - gs + groups, groups)]
    u = jnp.concatenate(
        [
            jnp.concatenate(
                [total[h * ELEM : (h + 1) * ELEM, c * LANES : (c + 1) * LANES] for h in range(wide)], axis=1
            )
            for c in range(3)
        ],
        axis=0,
    )
    for o in range(3 * ELEM):
        nodal[o : o + 1, :] = jnp.sum(flex[o] * u, axis=0, keepdims=True)

    per_row = LANES // ELEM
    own = iota((ELEM, LANES), 0) == (iota((ELEM, LANES), 1) >> log2(per_row))
    lines = []
    for c in range(3):
        for h in range(wide):
            lines.append(
                jnp.concatenate(
                    [
                        jnp.where(own, nodal[c * ELEM + i : c * ELEM + i + 1, h * LANES : (h + 1) * LANES], 0.0)
                        for i in range(ELEM)
                    ],
                    axis=1,
                )
            )
    lines = jnp.concatenate(lines, axis=0)
    k = iota((ELEM * LANES, LANES), 0)
    move = (k & (per_row - 1)) * ELEM + (k >> lane_shift)
    move = jnp.where(move == iota((ELEM * LANES, LANES), 1), 1.0, 0.0).astype(BF16)
    spread = 0.0
    for part in reversed(split(lines, 3)):
        spread = spread + jnp.dot(part, move, preferred_element_type=F32)
    for c in range(3):
        for h in range(highs):
            solid_s[c : c + 1, h * LANES : (h + 1) * LANES] = spread[c * highs + h : c * highs + h + 1, :]

    order = hist + 1
    solid = solid_s[...]
    residual = solid - disp[...]
    change = residual - rprev[...]
    with_change = vhist[0] * change[0:1, :]
    with_residual = vhist[0] * residual[0:1, :]
    for c in range(1, 3):
        with_change = with_change + vhist[c] * change[c : c + 1, :]
        with_residual = with_residual + vhist[c] * residual[c : c + 1, :]
    cross = jnp.sum(with_change, axis=1, keepdims=True)
    early = early + jnp.where(lane == hist, cross, 0.0)
    early = early + jnp.where(lane == order, jnp.sum(with_residual, axis=1, keepdims=True), 0.0)
    last = jnp.sum(jnp.where(lane == iota((hist, LANES), 0), cross, 0.0), axis=0, keepdims=True)
    lane_one = iota((1, LANES), 1)
    own_square = jnp.sum(jnp.sum(change * change, axis=0, keepdims=True), axis=1, keepdims=True)
    own_right = jnp.sum(jnp.sum(change * residual, axis=0, keepdims=True), axis=1, keepdims=True)
    last = last + jnp.where(lane_one == hist, own_square, 0.0) + jnp.where(lane_one == order, own_right, 0.0)
    grams[0, 0:hist, :] = early
    grams[0, hist : hist + 1, :] = last
    shares = [to_dev(3, grams.at[0], grams, b, b) for b in range(1, count)]
    for copy in shares:
        copy.start()
    image = solid - sprev[...]
    for copy in shares:
        copy.wait_recv()
    m = jnp.zeros((order, LANES), F32)
    for owner in range(count):
        m = m + grams[lax.rem(s - owner + count, count)]
    sub = iota(m.shape, 0)
    for k in range(order):
        row = m[k : k + 1, :] / m[k : k + 1, k : k + 1]
        m = jnp.where(sub == k, row, m - m[:, k : k + 1] * row)
    answer = m[:, order : order + 1]
    for c in range(3):
        old = jnp.sum(answer[0:hist, :] * whist[c], axis=0, keepdims=True)
        result[c : c + 1, :] = solid[c : c + 1, :] - answer[hist : hist + 1, :] * image[c : c + 1, :] - old
    store_result = pltpu.make_async_copy(result, updated_h, out_sems.at[1])
    store_result.start()
    for copy in asked + answers + pushed + shared + shares:
        copy.wait_send()
    pl.when(fluid)(store_fluid.wait)
    pl.when(jnp.logical_not(fluid))(store_state.wait)
    store_result.wait()


def per_device(
    sizes, fluid_state, coupling, displacement, slot_cells, slot_weights, slot_nodes, slot_counts,
    flexibility, resid_prev, struct_prev, v_hist, w_hist,
):
    groups, count = sizes
    comps, depth, width, span = fluid_state.shape[1:]
    capacity = slot_nodes.shape[-1]
    n_local = displacement.shape[1]
    order = v_hist.shape[0] + 1
    dma = pltpu.SemaphoreType.DMA
    vmem = pltpu.VMEM
    args = (
        fluid_state, coupling, displacement, slot_cells, slot_weights, slot_nodes, slot_counts, flexibility,
        resid_prev, struct_prev, v_hist.transpose(1, 0, 2), w_hist.transpose(1, 0, 2),
    )
    small = (1, 6)
    places = [(pltpu.SMEM if k in small else vmem)(a.shape, a.dtype) for k, a in enumerate(args)]
    hbm = pl.BlockSpec(memory_space=pltpu.HBM)
    halo = (2, 2, comps, depth, 1, span)
    slots = (count, 3, capacity)
    return pl.pallas_call(
        functools.partial(kernel, sizes),
        out_shape=(
            jax.ShapeDtypeStruct(fluid_state.shape, F32), jax.ShapeDtypeStruct(displacement.shape, F32),
        ),
        in_specs=[hbm] * len(args),
        out_specs=(hbm, hbm),
        scratch_shapes=places
        + [
            dma((len(args),)), dma((2,)), dma((4, count)), dma((4, count)), dma((groups,)), dma((groups,)),
            dma((2, 2)), dma((2, 2)),
            vmem((count, 1, capacity), jnp.int32), vmem((count, 1, capacity), jnp.int32),
            vmem(halo, F32), vmem(halo, F32),
            vmem((3 * n_local // LANES, LANES), F32), vmem(slots, F32), vmem(slots, F32), vmem(slots, F32),
            vmem((depth * width, 3 * span), F32),
            vmem((comps, depth, width, span), F32), vmem((comps, depth, width, span), F32),
            vmem((3 * span, 2 * depth * width), BF16),
            vmem(slots, F32), vmem(slots, F32), vmem((groups, n_local // LANES, 3 * LANES), F32),
            vmem((3 * ELEM, n_local // ELEM), F32), vmem((3, n_local), F32), vmem((count, order, LANES), F32),
            vmem((3, n_local), F32),
        ],
        compiler_params=pltpu.CompilerParams(
            collective_id=0, has_side_effects=True, vmem_limit_bytes=60 * 1024 * 1024
        ),
    )(*args)


def solution(mesh):
    sizes = (mesh.shape["group"], mesh.shape["dev"])
    return jax.shard_map(
        functools.partial(per_device, sizes),
        mesh=mesh,
        in_specs=(
            P("group", None, None, "dev", None),
            P(),
            P(None, "dev"),
            P("group", "dev", None, None, None),
            P("group", "dev", None, None, None),
            P("group", "dev", None, None),
            P("group", "dev", None),
            P(None, None, "dev"),
            P(None, "dev"),
            P(None, "dev"),
            P(None, None, "dev"),
            P(None, None, "dev"),
        ),
        out_specs=(P("group", None, None, "dev", None), P(None, "dev")),
        check_vma=False,
    )
```

time: 64.2 us -> 46.9 us (0.73)
  Pallas kernels: 53.7 us -> 42.7 us
  local copies, waits for them, and re-layouts: 9.1 us -> 3.35 us
    pallas_call x8 -> x1, Pallas kernels: 53.7 us -> 42.7 us  [per_device(): pl.pallas_call(functools.partial(kernel, sizes), out_shape=(jax.ShapeDtyp...]
    unnamed x41 -> x2, local copies, waits for them, and re-layouts: 9.1 us -> 3.35 us
where the time goes in v1:
time: 46.9 us; the launch traced here: 46.7 us
  Pallas kernels  42.7 us (91%)
  local copies, waits for them, and re-layouts  3.35 us (7%)
  between operations  0.64 us (1%)
    pallas_call x1, Pallas kernels, per_device(): pl.pallas_call(functools.partial(kernel, sizes), out_shape=(jax.ShapeDtyp...  42.7 us
    unnamed x2, local copies, waits for them, and re-layouts  3.35 us

profile of v1, /device:TPU:0, one launch (start us, length us, event | category | flops | bytes accessed | tf_op | source)
XLA Modules:
  0.0 46.7 jit_solution(11045126238325905371)
XLA Ops:
  0.6 42.7 %shard_map.131 = (f32[1,4,16,16,128]{4,3,2,1,0:T(8,128)}, f32[3,4096]{1,0:T(4,128)}) custom-call(f32[1,4,16,16,128]{4,3,2,1,0:T(8,128)} %state_h.1, f32[4,4]{1,0:T(4,128)} %coupling_h.1, f32[3,4096]{1,0:T(4,128)} %disp_h.1, s32[1,1,8,8,128]{4,3,2,1,0:T(8,128)} %cells_h.1, f32[1,1,8,8,128]{4,3,2,1,0:T(8,128)} %weights_h.1, s32[1,1,8,128]{3,2,1,0:T(8,128)} %nodes_h.1, ...), custom_call_target="tpu_custom_call" | custom-call | tf_op jit(solution)/shard_map/pallas_call | solution.py:426
  43.3 1.9 %copy.16 = f32[1,4,16,16,128]{4,3,2,1,0:T(8,128)} copy(f32[1,4,16,16,128]{4,3,2,1,0:T(8,128)} %get-tuple-element.4) | data formatting | bytes 1048576
  45.2 1.5 %copy.17 = f32[3,4096]{1,0:T(4,128)} copy(f32[3,4096]{1,0:T(4,128)} %get-tuple-element.5) | data formatting | bytes 98304

commit v2 on v1

--- a/solution.py
+++ b/solution.py
@@ -142,6 +142,18 @@
     return jnp.concatenate([jnp.where(mask, values[c : c + 1, :], 0.0).astype(BF16) for c in range(3)], axis=0)
 
 
+def scaled_columns(columns, values):
+    span, capacity = columns.shape
+    tile = 16
+    tiles = columns.reshape(span // tile, tile, capacity)
+    values = values.astype(F32)
+    out = []
+    for c in range(3):
+        row = jnp.broadcast_to(values[c : c + 1, :], (tile, capacity)).astype(BF16)
+        out.append((tiles * row[None]).reshape(span, capacity))
+    return jnp.concatenate(out, axis=0)
+
+
 def nt(left, right):
     return lax.dot_general(left, right, (((1,), (1,)), ((), ())), preferred_element_type=F32)
 
@@ -149,11 +161,11 @@
 def kernel(
     sizes,
     state_h, coupling_h, disp_h, cells_h, weights_h, nodes_h, counts_h, flex_h, rprev_h, sprev_h, vhist_h, whist_h,
-    fluid_h, updated_h,
+    fluid_o, result,
     state, coupling, disp, cells, weights, nodes, counts, flex, rprev, sprev, vhist, whist,
-    in_sems, out_sems, dev_send, dev_recv, group_send, group_recv, halo_send, halo_recv,
-    rows, table, edges, halos, flat, picked, arrived, masked, forcing, first, second, sampler,
-    force, forces, sums, nodal, solid_s, grams, result,
+    in_sems, dev_send, dev_recv, group_send, group_recv, halo_send, halo_recv,
+    rows, table, edges, halos, flat, picked, arrived, masked, forcing, first, second, sampler, row_hot, col_hot,
+    force, forces, sums, nodal, solid_s, grams,
 ):
     groups, count = sizes
     me = place()
@@ -189,6 +201,18 @@
     take_edges(state, (0,), edges.at[0])
     halo_copies(edges.at[0], halos.at[0], sizes, halo_send.at[0], halo_recv.at[0], "start")
     blank_ends(halos.at[0], sizes)
+
+    l_cells.wait()
+
+    def hot_corner(j, carry):
+        cell = cells[0, 0, j]
+        for p in range(count):
+            at = slice(p * capacity, (p + 1) * capacity)
+            row_hot[j, :, at] = hot(row_count, cell[p : p + 1, :] >> span_shift)
+            col_hot[j, :, at] = hot(span, cell[p : p + 1, :] & (span - 1))
+        return carry
+
+    lax.fori_loop(0, cells.shape[2], hot_corner, 0)
 
     l_disp.wait()
     for c in range(3):
@@ -218,7 +242,6 @@
     halo_copies(edges.at[0], halos.at[0], sizes, halo_send.at[0], halo_recv.at[0], "wait")
     add_halo(first, halos.at[0])
 
-    l_cells.wait()
     l_weights.wait()
     for copy in answers:
         copy.wait_recv()
@@ -227,16 +250,13 @@
     forcing[...] = jnp.zeros(forcing.shape, F32)
 
     def spread_corner(j, carry):
-        cell = cells[0, 0, j]
         weight = weights[0, 0, j]
-        left, high, low = [], [], []
+        high, low = [], []
         for p in range(count):
-            index = cell[p : p + 1, :]
-            left.append(hot(row_count, index >> span_shift))
-            mask = iota((span, capacity), 0) == (index & (span - 1))
+            columns = col_hot[j, :, p * capacity : (p + 1) * capacity]
             for into, part in zip((high, low), split(KAPPA * weight[p : p + 1, :] * masked[p], 2)):
-                into.append(spread_right(mask, part))
-        left = jnp.concatenate(left, axis=1)
+                into.append(scaled_columns(columns, part))
+        left = row_hot[j]
         both = nt(left, jnp.concatenate(high, axis=1)) + nt(left, jnp.concatenate(low, axis=1))
         forcing[...] += both
         return carry
@@ -262,10 +282,14 @@
     halo_copies(edges.at[1], halos.at[1], sizes, halo_send.at[1], halo_recv.at[1], "wait")
     add_halo(second, halos.at[1])
     fluid = g < groups - 1
-    store_fluid = pltpu.make_async_copy(second, fluid_h.at[0], out_sems.at[0])
-    store_state = pltpu.make_async_copy(state.at[0], fluid_h.at[0], out_sems.at[0])
-    pl.when(fluid)(store_fluid.start)
-    pl.when(jnp.logical_not(fluid))(store_state.start)
+
+    @pl.when(fluid)
+    def _():
+        fluid_o[0] = second[...]
+
+    @pl.when(jnp.logical_not(fluid))
+    def _():
+        fluid_o[...] = state[...]
 
     for c in range(3):
         for t, part in enumerate(split(second[c].reshape(row_count, span).T, 2)):
@@ -275,7 +299,7 @@
     def sample_corner(j, carry):
         cell = cells[0, 0, j]
         weight = weights[0, 0, j]
-        here = jnp.concatenate([hot(row_count, cell[p : p + 1, :] >> span_shift) for p in range(count)], axis=1)
+        here = row_hot[j]
         got = jnp.dot(sampler[...], jnp.concatenate([here, here], axis=0), preferred_element_type=F32)
         for p in range(count):
             mask = iota((span, capacity), 0) == (cell[p : p + 1, :] & (span - 1))
@@ -394,13 +418,18 @@
     for c in range(3):
         old = jnp.sum(answer[0:hist, :] * whist[c], axis=0, keepdims=True)
         result[c : c + 1, :] = solid[c : c + 1, :] - answer[hist : hist + 1, :] * image[c : c + 1, :] - old
-    store_result = pltpu.make_async_copy(result, updated_h, out_sems.at[1])
-    store_result.start()
     for copy in asked + answers + pushed + shared + shares:
         copy.wait_send()
-    pl.when(fluid)(store_fluid.wait)
-    pl.when(jnp.logical_not(fluid))(store_state.wait)
-    store_result.wait()
+
+
+def store_kernel(fluid_v, result_v, fluid_h, result_h, sems):
+    copies = [
+        pltpu.make_async_copy(fluid_v, fluid_h, sems.at[0]), pltpu.make_async_copy(result_v, result_h, sems.at[1]),
+    ]
+    for copy in copies:
+        copy.start()
+    for copy in copies:
+        copy.wait()
 
 
 def per_device(
@@ -423,16 +452,17 @@
     hbm = pl.BlockSpec(memory_space=pltpu.HBM)
     halo = (2, 2, comps, depth, 1, span)
     slots = (count, 3, capacity)
-    return pl.pallas_call(
+    shapes = (jax.ShapeDtypeStruct(fluid_state.shape, F32), jax.ShapeDtypeStruct(displacement.shape, F32))
+    local = pl.BlockSpec(memory_space=vmem)
+    corners = slot_cells.shape[2]
+    found = pl.pallas_call(
         functools.partial(kernel, sizes),
-        out_shape=(
-            jax.ShapeDtypeStruct(fluid_state.shape, F32), jax.ShapeDtypeStruct(displacement.shape, F32),
-        ),
+        out_shape=shapes,
         in_specs=[hbm] * len(args),
-        out_specs=(hbm, hbm),
+        out_specs=(local, local),
         scratch_shapes=places
         + [
-            dma((len(args),)), dma((2,)), dma((4, count)), dma((4, count)), dma((groups,)), dma((groups,)),
+            dma((len(args),)), dma((4, count)), dma((4, count)), dma((groups,)), dma((groups,)),
             dma((2, 2)), dma((2, 2)),
             vmem((count, 1, capacity), jnp.int32), vmem((count, 1, capacity), jnp.int32),
             vmem(halo, F32), vmem(halo, F32),
@@ -440,14 +470,17 @@
             vmem((depth * width, 3 * span), F32),
             vmem((comps, depth, width, span), F32), vmem((comps, depth, width, span), F32),
             vmem((3 * span, 2 * depth * width), BF16),
+            vmem((corners, depth * width, count * capacity), BF16), vmem((corners, span, count * capacity), BF16),
             vmem(slots, F32), vmem(slots, F32), vmem((groups, n_local // LANES, 3 * LANES), F32),
             vmem((3 * ELEM, n_local // ELEM), F32), vmem((3, n_local), F32), vmem((count, order, LANES), F32),
-            vmem((3, n_local), F32),
         ],
         compiler_params=pltpu.CompilerParams(
-            collective_id=0, has_side_effects=True, vmem_limit_bytes=60 * 1024 * 1024
+            collective_id=0, has_side_effects=True, vmem_limit_bytes=56 * 1024 * 1024
         ),
     )(*args)
+    return pl.pallas_call(
+        store_kernel, out_shape=shapes, in_specs=[local, local], out_specs=(hbm, hbm), scratch_shapes=[dma((2,))]
+    )(*found)
 
 
 def solution(mesh):

time: 46.9 us -> 45.1 us (0.962)
  local copies, waits for them, and re-layouts: 3.35 us -> 0 us
  Pallas kernels: 42.7 us -> 44.3 us
    unnamed x2 -> x0, local copies, waits for them, and re-layouts: 3.35 us -> none
    pallas_call x1 -> x2, Pallas kernels: 42.7 us -> 44.3 us  [the longest x1 42.4 us: per_device(): pl.pallas_call(functools.partial(kernel, sizes), out_shape=shapes, in_spe...]
where the time goes in v2:
time: 45.1 us; the launch traced here: 45 us
  Pallas kernels  44.3 us (98%)
  between operations  0.64 us (1%)
    pallas_call x1, Pallas kernels, per_device(): pl.pallas_call(functools.partial(kernel, sizes), out_shape=shapes, in_spe...  42.4 us
    pallas_call x1, Pallas kernels, per_device(): pl.pallas_call(store_kernel, out_shape=shapes, in_specs=[local, local], o...  1.86 us

profile of v2, /device:TPU:0, one launch (start us, length us, event | category | flops | bytes accessed | tf_op | source)
XLA Modules:
  0.0 45.0 jit_solution(648173653710967334)
XLA Ops:
  0.6 42.4 %shard_map.131 = (f32[1,4,16,16,128]{4,3,2,1,0:T(8,128)}, f32[3,4096]{1,0:T(4,128)}) custom-call(f32[1,4,16,16,128]{4,3,2,1,0:T(8,128)} %state_h.1, f32[4,4]{1,0:T(4,128)} %coupling_h.1, f32[3,4096]{1,0:T(4,128)} %disp_h.1, s32[1,1,8,8,128]{4,3,2,1,0:T(8,128)} %cells_h.1, f32[1,1,8,8,128]{4,3,2,1,0:T(8,128)} %weights_h.1, s32[1,1,8,128]{3,2,1,0:T(8,128)} %nodes_h.1, ...), custom_call_target="tpu_custom_call" | custom-call | tf_op jit(solution)/shard_map/pallas_call | solution.py:458
  43.1 1.9 %shard_map.132 = (f32[1,4,16,16,128]{4,3,2,1,0:T(8,128)}, f32[3,4096]{1,0:T(4,128)}) custom-call(f32[1,4,16,16,128]{4,3,2,1,0:T(8,128)} %get-tuple-element.4.fluid_v, f32[3,4096]{1,0:T(4,128)} %get-tuple-element.5.result_v), custom_call_target="tpu_custom_call" | custom-call | tf_op jit(solution)/shard_map/pallas_call | solution.py:481
